TPU v7x, 256 devices: a whole 4x4x8 slice. The times are simulated.
256 devices in a mesh: dp: 8 (over z), expert: 32 (over y, x, core).
Axes of the slice: x: 4, y: 4, z: 8, core: 2. Of those that a mesh axis runs over, the one named last changes fastest.
Arguments:
- tokens: bfloat16 [1024, 7168], P(('dp', 'expert')), may hold values from -6 to 6
- routes: int32 [1024, 8], P(('dp', 'expert')), may hold values from 0 to 31, all different within a row; in each aligned block of 4 rows (0 to 3, 4 to 7, ...) at most 2 rows name the same one
- gate_scores: float32 [1024, 8], P(('dp', 'expert')), may hold values from 0.1 to 1
- w_gate: bfloat16 [32, 7168, 2048], P('expert', None, 'dp'), may hold values from -0.0625 to 0.0625
- w_up: bfloat16 [32, 7168, 2048], P('expert', None, 'dp'), may hold values from -0.0625 to 0.0625
- w_down: bfloat16 [32, 2048, 7168], P('expert', 'dp'), may hold values from -0.125 to 0.125
Outputs:
- mixed_out: bfloat16 [1024, 7168], P(('dp', 'expert'))
Inputs may be any that keep to these rules, and one draw needn't show every extreme that they name: `routes`: each row names 8 different experts. In the rows of one device (aligned blocks of 4 rows) no expert is named by more than 2 rows, a bound that some block reaches.
All inputs are finite; a program needn't handle non-finite values.
Results may differ from a plain program's by a relative error of at most 0.0098.
Values may be sent and summed in bfloat16 or wider, within the bound.
No kernel may reach another device: no remote copies, remote signals or barrier semaphores. Data moves between devices by JAX's collectives and lax.ppermute only.
A program may use at most 128 MiB of HBM per device.

v0:
```python
import jax
import jax.numpy as jnp
from jax import lax
from jax.sharding import PartitionSpec as P


def slots_of(route_ids, owners):
    matched = (route_ids[:, None] == jnp.arange(owners, dtype=jnp.int32)[None, :]).astype(jnp.int32)
    before = jnp.cumsum(matched, axis=0) - matched
    return jnp.sum(before * matched, axis=1)


def expert_rows(picked_rows, gate_mat, up_mat, down_mat):
    gate_act = jnp.dot(picked_rows, gate_mat, preferred_element_type=jnp.float32)
    up_act = jnp.dot(picked_rows, up_mat, preferred_element_type=jnp.float32)
    hidden = (jax.nn.silu(gate_act) * up_act).astype(jnp.bfloat16)
    return jnp.dot(hidden, down_mat, preferred_element_type=jnp.float32)


def shards(tokens, routes, gate_scores, w_gate, w_up, w_down):
    tok_rows, model_width = tokens.shape
    route_count = routes.shape[1]
    owners = lax.axis_size("expert")
    capacity = tok_rows // 4 + 1
    gate_mat, up_mat, down_mat = (w_gate[0], w_up[0], w_down[0])
    source = jnp.repeat(jnp.arange(tok_rows, dtype=jnp.int32), route_count)
    flat_ids = routes.reshape(-1)
    own_slots = slots_of(flat_ids, owners)
    target_row = flat_ids * capacity + own_slots
    outgoing = (
        jnp.zeros((owners * capacity, model_width), jnp.bfloat16).at[target_row].set(tokens[source])
    )
    arrived = lax.all_to_all(
        outgoing.reshape(owners, capacity, model_width),
        "expert",
        split_axis=0,
        concat_axis=0,
        tiled=True,
    )
    blocks = lax.all_gather(arrived[None], "dp", axis=0, tiled=True)
    block_shape = blocks.shape[:-1] + (model_width,)
    flat_out = expert_rows(blocks.reshape(-1, model_width), gate_mat, up_mat, down_mat)
    partial_value = flat_out.reshape(block_shape)
    summed = lax.psum_scatter(
        partial_value.astype(jnp.bfloat16), "dp", scatter_dimension=0, tiled=True
    ).astype(jnp.float32)[0]
    returned = lax.all_to_all(
        summed.astype(jnp.bfloat16), "expert", split_axis=0, concat_axis=0, tiled=True
    ).astype(summed.dtype)
    lookup = flat_ids * capacity + own_slots
    picked = returned.reshape(owners * capacity, model_width)[lookup]
    mixed_out = jnp.sum(
        picked.reshape(tok_rows, route_count, model_width) * gate_scores[..., None], axis=1
    )
    return mixed_out.astype(jnp.bfloat16)


def solution(mesh):
    return jax.shard_map(
        shards,
        mesh=mesh,
        in_specs=(
            P(("dp", "expert"), None),
            P(("dp", "expert"), None),
            P(("dp", "expert"), None),
            P("expert", None, "dp"),
            P("expert", None, "dp"),
            P("expert", "dp", None),
        ),
        out_specs=P(("dp", "expert"), None),
        check_vma=False,
    )
```

profile of v0, /device:TPU:1, one launch (start us, length us, event | category | flops | bytes accessed | tf_op | source)
XLA Modules:
  0.0 270.3 jit_solution(8164090373457561248)
XLA Ops:
  6.5 0.8 eq.15
  7.3 0.7 broadcast_multiply_fusion
  8.0 0.1 fusion.16
  8.1 0.2 select_reduce_fusion
  8.3 0.1 mul.33
  8.4 0.1 reshape.80
  8.5 2.8 %scatter_custom_fusion = bf16[64,7168]{1,0:T(8,128)(2,1)S(1)} fusion(s32[32]{0:T(128)S(1)} %fusion.17, bf16[4,7168]{1,0:T(4,128)(2,1)S(1)} %copy-done, s32[1024]{0:T(1024)S(1)} %pad_clamp_fusion.1, bf16[]{:T(256)} %constant.7.clone.1), kind=kCustom, calls=%fused_computation.13 | custom fusion | bytes 917506 | tf_op jit(solution)/shard_map/scatter | solution.py:31
  11.4 0.3 reshape.81
  11.7 24.1 %all_to_all.10 = bf16[32,2,7168]{2,1,0:T(2,128)(2,1)} all-to-all(bf16[32,2,7168]{2,1,0:T(2,128)(2,1)S(1)} %reshape.81), channel_id=1, replica_groups=mesh['dp'=8,'expert'=32] {'expert'}, dimensions={0} | all-to-all | bytes 1835008 | tf_op jit(solution)/shard_map/all_to_all | solution.py:33
  35.9 0.2 reduce-scatter.2.cloned.1.call-start
  36.1 83.1 %all-gather.3.cloned.1.call-done = bf16[256,2,7168]{2,1,0:T(2,128)(2,1)} async-done(((bf16[32,2,7168]{2,1,0:T(2,128)(2,1)}), bf16[256,2,7168]{2,1,0:T(2,128)(2,1)}) %all-gather.3.cloned.1.call-update) | async-done | bytes 7340048 | tf_op jit(solution)/shard_map/all_gather | solution.py:40
  119.2 15.4 %reshape.82 = bf16[512,7168]{1,0:T(8,128)(2,1)} reshape(bf16[256,2,7168]{2,1,0:T(2,128)(2,1)} %all-gather.3.cloned.1.call-done) | data formatting | bytes 14680064 | tf_op jit(solution)/shard_map/reshape | solution.py:42
  134.6 6.3 %fusion.3 = f32[512,256]{1,0:T(8,128)S(1)} fusion(bf16[512,7168]{1,0:T(8,128)(2,1)} %reshape.82, bf16[1,7168,256]{2,1,0:T(8,128)(2,1)} %param.9), kind=kOutput, calls=%fused_computation.7 | convolution fusion | flops 1879048192 | bytes 11534336 | tf_op jit(solution)/shard_map/dot_general | solution.py:14
  141.0 0.9 copy-done.3
  141.9 2.1 fusion.8
  143.9 0.1 dot_general.13
  144.0 7.1 %convolution_convert_fusion = bf16[8,32,2,7168]{3,1,2,0:T(8,128)(2,1)} fusion(bf16[1,256,7168]{2,1,0:T(8,128)(2,1)} %param.11, bf16[8,32,2,256]{3,2,1,0:T(2,128)(2,1)S(1)} %dot_general.13), kind=kOutput, calls=%fused_computation.3 | convolution fusion | flops 1882718208 | bytes 11272192 | tf_op jit(solution)/shard_map/dot_general | solution.py:17
  151.2 83.9 %reduce-scatter.2.cloned.1.call-done = bf16[1,32,2,7168]{3,1,2,0:T(8,128)(2,1)} async-done(((bf16[8,32,2,7168]{3,1,2,0:T(8,128)(2,1)}), bf16[1,32,2,7168]{3,1,2,0:T(8,128)(2,1)}) %reduce-scatter.2.cloned.1.call-update) | async-done | bytes 917520 | tf_op jit(solution)/shard_map/reduce_scatter | solution.py:44
  235.1 3.0 %copy.11 = bf16[32,2,7168]{2,1,0:T(2,128)(2,1)} copy(bf16[32,2,7168]{2,0,1:T(8,128)(2,1)} %bitcast.32) | data formatting | bytes 1835008 | tf_op jit(solution)/shard_map/convert_element_type | solution.py:48
  238.1 7.6 %all-to-all-start.1 = ((bf16[32,2,7168]{2,1,0:T(2,128)(2,1)}), bf16[32,2,7168]{2,1,0:T(2,128)(2,1)S(1)}, u32[]{:S(2)}, u32[]{:S(2)}) async-start(bf16[32,2,7168]{2,1,0:T(2,128)(2,1)} %copy.11), calls=%async_computation.2 | async-start | bytes 1835008 | tf_op jit(solution)/shard_map/all_to_all | solution.py:47
  245.7 15.6 %all-to-all-done.1 = bf16[32,2,7168]{2,1,0:T(2,128)(2,1)S(1)} async-done(((bf16[32,2,7168]{2,1,0:T(2,128)(2,1)}), bf16[32,2,7168]{2,1,0:T(2,128)(2,1)S(1)}, u32[]{:S(2)}, u32[]{:S(2)}) %all-to-all-start.1) | async-done | bytes 917536 | tf_op jit(solution)/shard_map/all_to_all | solution.py:47
  261.3 0.3 reshape.87
  261.6 0.9 gather_fusion
  262.5 1.0 fusion.11
  (16 shorter events, 0.1 us)
Async XLA Ops:
  6.5 2.0 copy-start
  6.5 112.6 %all-gather.3.cloned.1.call-start = ((), (), s32[]{:S(2)}) async-start(), calls=%async_computation.4 | async-start | bytes 8257536 | tf_op jit(solution)/shard_map/all_gather | solution.py:40
  35.9 199.2 %reduce-scatter.2.cloned.1.call-start = ((), (), s32[]{:S(2)}) async-start(), calls=%async_computation.3 | async-start | bytes 8257536 | tf_op jit(solution)/shard_map/reduce_scatter | solution.py:44
  134.6 6.3 %copy-start.1 = (bf16[512,7168]{1,0:T(8,128)(2,1)S(1)}, bf16[512,7168]{1,0:T(8,128)(2,1)}, u32[]{:S(2)}) copy-start(bf16[512,7168]{1,0:T(8,128)(2,1)} %reshape.82) | copy-start | bytes 22020100
  134.6 7.3 %copy-start.3 = (bf16[1,7168,256]{2,1,0:T(8,128)(2,1)S(1)}, bf16[1,7168,256]{2,1,0:T(8,128)(2,1)}, u32[]{:S(2)}) copy-start(bf16[1,7168,256]{2,1,0:T(8,128)(2,1)} %param.10) | copy-start | bytes 11010052
  238.1 23.2 %all-to-all-start.1 = ((bf16[32,2,7168]{2,1,0:T(2,128)(2,1)}), bf16[32,2,7168]{2,1,0:T(2,128)(2,1)S(1)}, u32[]{:S(2)}, u32[]{:S(2)}) async-start(bf16[32,2,7168]{2,1,0:T(2,128)(2,1)} %copy.11), calls=%async_computation.2 | async-start | bytes 1835008 | tf_op jit(solution)/shard_map/all_to_all | solution.py:47
  261.6 0.9 copy-start.2
Sparse Core Ops, SparseCore 0:
  36.0 83.1 all-gather.2
  151.3 83.7 reduce-scatter.1
where the time goes:
time: 271 us; the launch traced here: 270 us
  waiting for transfers between devices  183 us (68%)
  local copies, waits for them, and re-layouts  24.7 us (9%)
  blocking collectives  24.1 us (9%)
  matrix products  15.5 us (6%)
  between operations  13.5 us (5%)
  starting transfers between devices  7.81 us (3%)
    reduce_scatter x1, waiting for transfers between devices, shards(): lax.psum_scatter(partial_value.astype(jnp.bfloat16), 'dp', scatter_dimens...  83.9 us
    all_gather x1, waiting for transfers between devices, shards(): blocks = lax.all_gather(arrived[None], 'dp', axis=0, tiled=True)  83.1 us
    all_to_all x1, blocking collectives, shards(): lax.all_to_all(outgoing.reshape(owners, capacity, model_width), 'expert',...  24.1 us
    all_to_all x1, waiting for transfers between devices, shards(): lax.all_to_all(summed.astype(jnp.bfloat16), 'expert', split_axis=0, conca...  15.6 us
    reshape x1, local copies, waits for them, and re-layouts, shards(): blocks.reshape(-1, model_width)  15.4 us
    all_to_all x1, starting transfers between devices, shards(): lax.all_to_all(summed.astype(jnp.bfloat16), 'expert', split_axis=0, conca...  7.59 us
    dot_general x1, matrix products, expert_rows(): return jnp.dot(hidden, down_mat, preferred_element_type=jnp.float32)  7.1 us
    dot_general x1, matrix products, expert_rows(): jnp.dot(picked_rows, gate_mat, preferred_element_type=jnp.float32)  6.33 us
  transfers between devices with their start and end apart: 3, of which 3 were waited for; matrix products, arithmetic and copies ran while one was open for 0% of the time, Pallas kernels for 0%

commit v1 on v0

--- a/solution.py
+++ b/solution.py
@@ -2,6 +2,12 @@
 import jax.numpy as jnp
 from jax import lax
 from jax.sharding import PartitionSpec as P
+
+
+def gather_from_all(x, axis, dim):
+    devices = lax.axis_size(axis)
+    repeats = [devices if d == dim else 1 for d in range(x.ndim)]
+    return lax.all_to_all(jnp.tile(x, repeats), axis, split_axis=dim, concat_axis=dim, tiled=True)
 
 
 def slots_of(route_ids, owners):
@@ -37,7 +43,7 @@
         concat_axis=0,
         tiled=True,
     )
-    blocks = lax.all_gather(arrived[None], "dp", axis=0, tiled=True)
+    blocks = gather_from_all(arrived[None], "dp", 0)
     block_shape = blocks.shape[:-1] + (model_width,)
     flat_out = expert_rows(blocks.reshape(-1, model_width), gate_mat, up_mat, down_mat)
     partial_value = flat_out.reshape(block_shape)

time: 271 us -> 359 us (1.32)
  blocking collectives: 24.1 us -> 195 us
  waiting for transfers between devices: 183 us -> 95 us
  local copies, waits for them, and re-layouts: 24.7 us -> 29.7 us
    all_to_all x0 -> x1, blocking collectives: none -> 171 us  [gather_from_all(): lax.all_to_all(jnp.tile(x, repeats), axis, split_axis=dim, concat_axis=di...]
    all_gather x1 -> x0, waiting for transfers between devices: 83.1 us -> none  [shards(): blocks = lax.all_gather(arrived[None], 'dp', axis=0, tiled=True)]
    another operation x0 -> x1, local copies, waits for them, and re-layouts: none -> 4.95 us  [gather_from_all(): jnp.tile(x, repeats)]
    reduce_scatter x1, waiting for transfers between devices: 83.9 us -> 79.4 us  [shards(): lax.psum_scatter(partial_value.astype(jnp.bfloat16), 'dp', scatter_dimens...]
  transfers between devices with their start and end apart: 3 -> 2, of which waited for: 3 -> 2; matrix products, arithmetic and copies ran while one was open for 0% -> 0% of each run, Pallas kernels for 0% -> 0%
where the time goes in v1:
time: 359 us; the launch traced here: 358 us
  blocking collectives  195 us (54%)
  waiting for transfers between devices  95 us (26%)
  local copies, waits for them, and re-layouts  29.7 us (8%)
  matrix products  15.5 us (4%)
  between operations  13.5 us (4%)
  starting transfers between devices  7.6 us (2%)
    all_to_all x1, blocking collectives, gather_from_all(): lax.all_to_all(jnp.tile(x, repeats), axis, split_axis=dim, concat_axis=di...  171 us
    reduce_scatter x1, waiting for transfers between devices, shards(): lax.psum_scatter(partial_value.astype(jnp.bfloat16), 'dp', scatter_dimens...  79.4 us
    all_to_all x1, blocking collectives, shards(): lax.all_to_all(outgoing.reshape(owners, capacity, model_width), 'expert',...  24 us
    all_to_all x1, waiting for transfers between devices, shards(): lax.all_to_all(summed.astype(jnp.bfloat16), 'expert', split_axis=0, conca...  15.6 us
    reshape x1, local copies, waits for them, and re-layouts, shards(): blocks.reshape(-1, model_width)  15.4 us
    all_to_all x1, starting transfers between devices, shards(): lax.all_to_all(summed.astype(jnp.bfloat16), 'expert', split_axis=0, conca...  7.59 us
  transfers between devices with their start and end apart: 2, of which 2 were waited for; matrix products, arithmetic and copies ran while one was open for 0% of the time, Pallas kernels for 0%

profile of v1, /device:TPU:1, one launch (start us, length us, event | category | flops | bytes accessed | tf_op | source)
XLA Modules:
  0.0 358.0 jit_solution(7936554085524825750)
XLA Ops:
  6.5 0.8 eq.15
  7.3 0.7 broadcast_multiply_fusion
  8.0 0.1 fusion.16
  8.1 0.2 select_reduce_fusion
  8.3 0.1 mul.33
  8.4 0.1 reshape.83
  8.5 2.8 scatter_custom_fusion
  11.4 0.3 reshape.84
  11.7 24.0 %all_to_all.15 = bf16[32,2,7168]{2,1,0:T(2,128)(2,1)S(1)} all-to-all(bf16[32,2,7168]{2,1,0:T(2,128)(2,1)S(1)} %reshape.84), channel_id=1, replica_groups=mesh['dp'=8,'expert'=32] {'expert'}, dimensions={0} | all-to-all | bytes 1835008 | tf_op jit(solution)/shard_map/all_to_all | solution.py:39
  35.7 4.9 %tile.2 = bf16[8,32,2,7168]{3,2,1,0:T(2,128)(2,1)S(1)} broadcast(bf16[32,2,7168]{2,1,0:T(2,128)(2,1)S(1)} %all_to_all.15), dimensions={1,2,3} | broadcast | bytes 8257536 | tf_op jit(solution)/shard_map/tile | solution.py:10
  40.7 170.6 %all_to_all.16 = bf16[8,32,2,7168]{3,2,1,0:T(2,128)(2,1)} all-to-all(bf16[8,32,2,7168]{3,2,1,0:T(2,128)(2,1)S(1)} %tile.2), channel_id=1, replica_groups=mesh['dp'=8,'expert'=32] {'dp'}, dimensions={0} | all-to-all | bytes 14680064 | tf_op jit(solution)/shard_map/all_to_all | solution.py:10
  211.3 15.4 %reshape.85 = bf16[512,7168]{1,0:T(8,128)(2,1)} reshape(bf16[8,32,2,7168]{3,2,1,0:T(2,128)(2,1)} %all_to_all.16) | data formatting | bytes 14680064 | tf_op jit(solution)/shard_map/reshape | solution.py:48
  226.8 6.3 %fusion.3 = f32[512,256]{1,0:T(8,128)S(1)} fusion(bf16[512,7168]{1,0:T(8,128)(2,1)} %reshape.85, bf16[1,7168,256]{2,1,0:T(8,128)(2,1)} %param.9), kind=kOutput, calls=%fused_computation.7 | convolution fusion | flops 1879048192 | bytes 11534336 | tf_op jit(solution)/shard_map/dot_general | solution.py:20
  233.1 0.9 copy-done.3
  234.0 2.1 fusion.8
  236.1 0.1 dot_general.13
  236.2 7.1 %convolution_convert_fusion = bf16[8,32,2,7168]{3,1,2,0:T(8,128)(2,1)} fusion(bf16[1,256,7168]{2,1,0:T(8,128)(2,1)} %param.11, bf16[8,32,2,256]{3,2,1,0:T(2,128)(2,1)S(1)} %dot_general.13), kind=kOutput, calls=%fused_computation.3 | convolution fusion | flops 1882718208 | bytes 11272192 | tf_op jit(solution)/shard_map/dot_general | solution.py:23
  243.3 79.4 %reduce-scatter.2.cloned.1.call-done = bf16[1,32,2,7168]{3,1,2,0:T(8,128)(2,1)} async-done(((bf16[8,32,2,7168]{3,1,2,0:T(8,128)(2,1)}), bf16[1,32,2,7168]{3,1,2,0:T(8,128)(2,1)}) %reduce-scatter.2.cloned.1.call-update) | async-done | bytes 917520 | tf_op jit(solution)/shard_map/reduce_scatter | solution.py:50
  322.7 3.0 copy.11
  325.7 7.6 %all-to-all-start.2 = ((bf16[32,2,7168]{2,1,0:T(2,128)(2,1)}), bf16[32,2,7168]{2,1,0:T(2,128)(2,1)S(1)}, u32[]{:S(2)}, u32[]{:S(2)}) async-start(bf16[32,2,7168]{2,1,0:T(2,128)(2,1)} %copy.11), calls=%async_computation.3 | async-start | bytes 1835008 | tf_op jit(solution)/shard_map/all_to_all | solution.py:53
  333.4 15.6 %all-to-all-done.2 = bf16[32,2,7168]{2,1,0:T(2,128)(2,1)S(1)} async-done(((bf16[32,2,7168]{2,1,0:T(2,128)(2,1)}), bf16[32,2,7168]{2,1,0:T(2,128)(2,1)S(1)}, u32[]{:S(2)}, u32[]{:S(2)}) %all-to-all-start.2) | async-done | bytes 917536 | tf_op jit(solution)/shard_map/all_to_all | solution.py:53
  349.0 0.3 reshape.90
  349.3 0.9 gather_fusion
  350.1 1.0 fusion.11
  (15 shorter events, 0.1 us)
Async XLA Ops:
  6.5 2.0 copy-start
  6.5 316.2 %reduce-scatter.2.cloned.1.call-start = ((), (), s32[]{:S(2)}) async-start(), calls=%async_computation.4 | async-start | bytes 8257536 | tf_op jit(solution)/shard_map/reduce_scatter | solution.py:50
  226.8 6.3 %copy-start.1 = (bf16[512,7168]{1,0:T(8,128)(2,1)S(1)}, bf16[512,7168]{1,0:T(8,128)(2,1)}, u32[]{:S(2)}) copy-start(bf16[512,7168]{1,0:T(8,128)(2,1)} %reshape.85) | copy-start | bytes 22020100
  226.8 7.3 %copy-start.3 = (bf16[1,7168,256]{2,1,0:T(8,128)(2,1)S(1)}, bf16[1,7168,256]{2,1,0:T(8,128)(2,1)}, u32[]{:S(2)}) copy-start(bf16[1,7168,256]{2,1,0:T(8,128)(2,1)} %param.10) | copy-start | bytes 11010052
  325.7 23.2 %all-to-all-start.2 = ((bf16[32,2,7168]{2,1,0:T(2,128)(2,1)}), bf16[32,2,7168]{2,1,0:T(2,128)(2,1)S(1)}, u32[]{:S(2)}, u32[]{:S(2)}) async-start(bf16[32,2,7168]{2,1,0:T(2,128)(2,1)} %copy.11), calls=%async_computation.3 | async-start | bytes 1835008 | tf_op jit(solution)/shard_map/all_to_all | solution.py:53
  349.3 0.9 copy-start.2
Sparse Core Ops, SparseCore 0:
  243.4 79.2 reduce-scatter.1
